TPU v7x, 32 devices: a whole 2x2x4 slice. The times are simulated.
32 devices in a mesh: smp: 8 (over z, y), var: 4 (over x, core).
Axes of the slice: x: 2, y: 2, z: 4, core: 2. Of those that a mesh axis runs over, the one named last changes fastest.
Arguments:
- dosage: int32 [512, 2048], P('smp', 'var'), may hold values from -2147483648 to 2147483647, as said below
- shares_init: float32 [12, 8192], P(None, ('smp', 'var')), may hold values from 0.1 to 1
- freqs_init: float32 [12, 2048], P(None, ('var', 'smp')), may hold values from 0.019 to 0.981
Outputs:
- shares: float32 [12, 8192], P(None, ('smp', 'var'))
- freqs: float32 [12, 2048], P(None, ('var', 'smp'))
Inputs may be any that keep to these rules, and one draw needn't show every extreme that they name: Every 2-bit code in a word of dosage is 0, 1, 2 or 3, and 3 marks a missing genotype.
All inputs are finite; a program needn't handle non-finite values.
Results may differ from a plain program's by a relative error of at most 0.0003.
Values sent between devices are 32-bit elements; how exact they have to be, the bound alone decides.
A program may use at most 64 MiB of HBM per device.

v0:
```python
import jax
import jax.numpy as jnp
from jax import lax
from jax.sharding import PartitionSpec as P

ITERS = 2
HIGH = lax.Precision.HIGHEST


def unpack_codes(packed):
    shifts = 2 * jnp.arange(16, dtype=jnp.int32)
    codes = jnp.bitwise_and(jnp.right_shift(packed[:, None, :], shifts[None, :, None]), 3)
    return codes.reshape(packed.shape[0] * 16, packed.shape[1])


def expect_sums(packed, shares_block, freqs_block):
    codes = unpack_codes(packed)
    live = (codes < 3).astype(jnp.float32)
    allele_f = live * codes.astype(jnp.float32)
    probs = jnp.einsum("kn,km->nm", shares_block, freqs_block, precision=HIGH)
    ratio_alt = allele_f / probs
    ratio_ref = (2.0 * live - allele_f) / (1.0 - probs)
    sum_q = jnp.einsum("km,nm->kn", freqs_block, ratio_alt, precision=HIGH) + jnp.einsum(
        "km,nm->kn", 1.0 - freqs_block, ratio_ref, precision=HIGH
    )
    sum_a = jnp.einsum("kn,nm->km", shares_block, ratio_alt, precision=HIGH)
    sum_b = jnp.einsum("kn,nm->km", shares_block, ratio_ref, precision=HIGH)
    return (sum_q, sum_a, sum_b)


def block_sums(packed, shares_block, freqs_block):
    word_rows = min(packed.shape[0], 16)
    blocks = packed.shape[0] // word_rows
    populations = shares_block.shape[0]
    packed_blocks = packed.reshape(blocks, word_rows, packed.shape[1])
    share_blocks = shares_block.reshape(populations, blocks, word_rows * 16).transpose(1, 0, 2)

    def one_block(carry, items):
        sum_q, sum_a, sum_b = expect_sums(items[0], items[1], freqs_block)
        return ((carry[0] + sum_a, carry[1] + sum_b), sum_q)

    start = (jnp.zeros(freqs_block.shape, jnp.float32), jnp.zeros(freqs_block.shape, jnp.float32))
    totals, sums_q = lax.scan(one_block, start, (packed_blocks, share_blocks))
    sum_q = sums_q.transpose(1, 0, 2).reshape(populations, shares_block.shape[1])
    return (sum_q, totals[0], totals[1])


def renew_shares(shares_block, sum_q):
    numer = shares_block * sum_q
    return (numer + 0.5) / (jnp.sum(numer, axis=0, keepdims=True) + 0.5 * shares_block.shape[0])


def renew_freqs(freqs_block, sum_a, sum_b):
    alt_part = freqs_block * sum_a
    ref_part = (1.0 - freqs_block) * sum_b
    return (alt_part + 0.5) / (alt_part + ref_part + 1.0)


def body(dosage, shares_init, freqs_init):
    own_shares = shares_init / jnp.sum(shares_init, axis=0, keepdims=True)
    own_freqs = freqs_init
    share_width = shares_init.shape[1]
    freq_width = freqs_init.shape[1]
    shares_block = lax.all_gather(own_shares, "var", axis=1, tiled=True)
    freqs_block = lax.all_gather(own_freqs, "smp", axis=1, tiled=True)
    for iteration in range(ITERS):
        part_q, part_a, part_b = block_sums(dosage, shares_block, freqs_block)
        sum_q = lax.psum(part_q, "var")
        sum_a, sum_b = lax.psum((part_a, part_b), "smp")
        shares_block = renew_shares(shares_block, sum_q)
        freqs_block = renew_freqs(freqs_block, sum_a, sum_b)
        if iteration + 1 == ITERS:
            own_shares = lax.dynamic_slice_in_dim(
                shares_block, lax.axis_index("var") * share_width, share_width, 1
            )
            own_freqs = lax.dynamic_slice_in_dim(
                freqs_block, lax.axis_index("smp") * freq_width, freq_width, 1
            )
    return (own_shares, own_freqs)


def solution(mesh):
    placed = (P("smp", "var"), P(None, ("smp", "var")), P(None, ("var", "smp")))
    return jax.shard_map(
        body,
        mesh=mesh,
        in_specs=placed,
        out_specs=(P(None, ("smp", "var")), P(None, ("var", "smp"))),
        check_vma=False,
    )
```

profile of v0, /device:TPU:0, one launch (start us, length us, event | category | flops | bytes accessed | tf_op | source)
XLA Modules:
  0.0 156.3 jit_solution(4070201371241163746)
XLA Ops:
  0.6 0.8 reduce_sum.27
  1.4 6.2 %all_gather.6 = f32[12,1024]{1,0:T(8,128)S(1)} all-gather(f32[12,256]{1,0:T(8,128)S(1)} %broadcast_divide_fusion), channel_id=1, replica_groups=mesh['smp'=8,'var'=4] {'var'}, dimensions={1}, use_global_device_ids=true | all-gather | bytes 61440 | tf_op jit(solution)/shard_map/all_gather | solution.py:64
  7.7 0.7 copy-done.2
  8.4 31.4 %all-gather = f32[8,64,12]{1,2,0:T(8,128)S(1)} all-gather(f32[1,64,12]{1,2,0:T(8,128)S(1)} %bitcast.171), channel_id=1, replica_groups=mesh['smp'=8,'var'=4] {'smp'}, dimensions={0}, use_global_device_ids=true | all-gather | bytes 27648 | tf_op jit(solution)/shard_map/all_gather | solution.py:65
  39.9 0.8 copy-done
  40.7 10.8 %while.30 = (s32[]{:T(128)}, f32[12,512]{1,0:T(8,128)S(1)}, f32[12,512]{1,0:T(8,128)S(1)}, f32[4,12,256]{2,1,0:T(8,128)S(1)}, f32[4,12,256]{2,1,0:T(8,128)S(1)},...) while((s32[]{:T(128)}, f32[12,512]{1,0:T(8,128)S(1)}, ...), condition=%wide.region_2.3_spmd.clone, body=%wide.region_1.2_spmd.clone.sunk | while | flops 95716368 | bytes 3547396 | solution.py:43
  40.8 0.8 fusion.92
  41.6 0.4 convolution_add_fusion.10
  41.9 0.4 convolution_add_fusion.11
  42.3 0.5 convolution_bitcast_fusion.4
  42.8 0.5 fusion.93
  43.5 0.8 fusion.92
  44.2 0.4 convolution_add_fusion.10
  44.6 0.4 convolution_add_fusion.11
  45.0 0.5 convolution_bitcast_fusion.4
  45.5 0.5 fusion.93
  46.2 0.8 fusion.92
  46.9 0.4 convolution_add_fusion.10
  47.3 0.4 convolution_add_fusion.11
  47.7 0.5 convolution_bitcast_fusion.4
  48.2 0.5 fusion.93
  48.8 0.8 fusion.92
  49.6 0.4 convolution_add_fusion.10
  50.4 0.5 convolution_bitcast_fusion.4
  50.9 0.5 fusion.93
  51.5 10.7 %psum.42 = f32[12,1024]{1,0:T(8,128)S(1)} all-reduce(f32[12,1024]{1,0:T(8,128)S(1)} %bitcast.169), channel_id=1, replica_groups=mesh['smp'=8,'var'=4] {'var'}, use_global_device_ids=true, to_apply=%region_3.4 | all-reduce | flops 12288 | bytes 98304 | tf_op jit(solution)/shard_map/psum | solution.py:68
  62.3 37.5 %all-reduce.1 = (f32[12,512]{1,0:T(8,128)S(1)}, f32[12,512]{1,0:T(8,128)S(1)}) all-reduce(f32[12,512]{1,0:T(8,128)S(1)} %get-tuple-element.82, f32[12,512]{1,0:T(8,128)S(1)} %get-tuple-element.81), channel_id=1, replica_groups=mesh['smp'=8,'var'=4] {'smp'}, use_global_device_ids=true, to_apply=%region_6.7 | all-reduce | flops 12288 | bytes 98304 | tf_op jit(solution)/shard_map/psum | solution.py:69
  99.9 10.8 %while.31 = (s32[]{:T(128)}, f32[12,512]{1,0:T(8,128)S(1)}, f32[12,512]{1,0:T(8,128)S(1)}, f32[4,12,256]{2,1,0:T(8,128)S(1)}, f32[4,12,256]{2,1,0:T(8,128)S(1)},...) while((s32[]{:T(128)}, f32[12,512]{1,0:T(8,128)S(1)}, ...), condition=%wide.region_8.9_spmd.clone, body=%wide.region_7.8_spmd.clone.sunk | while | flops 95716368 | bytes 3547396 | solution.py:43
  100.0 0.8 fusion.103
  100.8 0.4 convolution_add_fusion.12
  101.5 0.5 convolution_bitcast_fusion.5
  102.1 0.5 fusion.104
  102.7 0.8 fusion.103
  103.5 0.4 convolution_add_fusion.12
  104.2 0.5 convolution_bitcast_fusion.5
  104.8 0.5 fusion.104
  105.4 0.8 fusion.103
  106.2 0.4 convolution_add_fusion.12
  106.9 0.5 convolution_bitcast_fusion.5
  107.5 0.5 fusion.104
  108.1 0.8 fusion.103
  108.9 0.4 convolution_add_fusion.12
  109.6 0.5 convolution_bitcast_fusion.5
  110.2 0.5 fusion.104
  110.8 10.7 %psum.45 = f32[12,1024]{1,0:T(8,128)S(1)} all-reduce(f32[12,1024]{1,0:T(8,128)S(1)} %bitcast.170), channel_id=1, replica_groups=mesh['smp'=8,'var'=4] {'var'}, use_global_device_ids=true, to_apply=%region_9.10 | all-reduce | flops 12288 | bytes 98304 | tf_op jit(solution)/shard_map/psum | solution.py:68
  121.6 0.6 fusion.44
  122.2 33.4 %all-reduce = (f32[12,512]{1,0:T(8,128)S(1)}, f32[12,512]{1,0:T(8,128)S(1)}) all-reduce(f32[12,512]{1,0:T(8,128)S(1)} %get-tuple-element.85, f32[12,512]{1,0:T(8,128)S(1)} %get-tuple-element.84), channel_id=1, replica_groups=mesh['smp'=8,'var'=4] {'smp'}, use_global_device_ids=true, to_apply=%region_12.13 | all-reduce | flops 12288 | bytes 98304 | tf_op jit(solution)/shard_map/psum | solution.py:69
  155.6 0.7 fusion.47
  (67 shorter events, 3.1 us)
Async XLA Ops:
  0.6 0.8 copy-start.1
  7.7 0.7 copy-start.2
  39.8 0.9 copy-start
where the time goes:
time: 157 us; the launch traced here: 156 us
  blocking collectives  130 us (83%)
  matrix products  20.5 us (13%)
  local copies, waits for them, and re-layouts  2.55 us (2%)
  other arithmetic  2.3 us (1%)
    psum x2, blocking collectives, body(): sum_a, sum_b = lax.psum((part_a, part_b), 'smp')  70.9 us
    all_gather x1, blocking collectives, body(): freqs_block = lax.all_gather(own_freqs, 'smp', axis=1, tiled=True)  31.4 us
    psum x2, blocking collectives, body(): sum_q = lax.psum(part_q, 'var')  21.3 us
    dot_general x8, matrix products, expect_sums(): probs = jnp.einsum('kn,km->nm', shares_block, freqs_block, precision=HIGH)  6.22 us
    all_gather x1, blocking collectives, body(): shares_block = lax.all_gather(own_shares, 'var', axis=1, tiled=True)  6.22 us
    dot_general x8, matrix products, expect_sums(): jnp.einsum('km,nm->kn', 1.0 - freqs_block, ratio_ref, precision=HIGH)  4.22 us
    dot_general x8, matrix products, expect_sums(): jnp.einsum('km,nm->kn', freqs_block, ratio_alt, precision=HIGH)  4.14 us

commit v1 on v0

--- a/solution.py
+++ b/solution.py
@@ -65,7 +65,7 @@
     freqs_block = lax.all_gather(own_freqs, "smp", axis=1, tiled=True)
     for iteration in range(ITERS):
         part_q, part_a, part_b = block_sums(dosage, shares_block, freqs_block)
-        sum_q = lax.psum(part_q, "var")
+        sum_q = jnp.sum(lax.all_gather(part_q, "var"), axis=0)
         sum_a, sum_b = lax.psum((part_a, part_b), "smp")
         shares_block = renew_shares(shares_block, sum_q)
         freqs_block = renew_freqs(freqs_block, sum_a, sum_b)

time: 157 us -> 147 us (0.936)
  blocking collectives: 130 us -> 120 us
    psum x2 -> x0, blocking collectives: 21.3 us -> none  [body(): sum_q = lax.psum(part_q, 'var')]
    all_gather x0 -> x2, blocking collectives: none -> 11.6 us  [body(): sum_q = jnp.sum(lax.all_gather(part_q, 'var'), axis=0)]
where the time goes in v1:
time: 147 us
  blocking collectives  120 us (82%)
  matrix products  20.5 us (14%)
  local copies, waits for them, and re-layouts  2.55 us (2%)
  other arithmetic  2.33 us (2%)
    psum x2, blocking collectives, body(): sum_a, sum_b = lax.psum((part_a, part_b), 'smp')  70.9 us
    all_gather x1, blocking collectives, body(): freqs_block = lax.all_gather(own_freqs, 'smp', axis=1, tiled=True)  31.4 us
    all_gather x2, blocking collectives, body(): sum_q = jnp.sum(lax.all_gather(part_q, 'var'), axis=0)  11.6 us
    dot_general x8, matrix products, expect_sums(): probs = jnp.einsum('kn,km->nm', shares_block, freqs_block, precision=HIGH)  6.22 us
    all_gather x1, blocking collectives, body(): shares_block = lax.all_gather(own_shares, 'var', axis=1, tiled=True)  6.22 us
    dot_general x8, matrix products, expect_sums(): jnp.einsum('km,nm->kn', 1.0 - freqs_block, ratio_ref, precision=HIGH)  4.22 us
    dot_general x8, matrix products, expect_sums(): jnp.einsum('km,nm->kn', freqs_block, ratio_alt, precision=HIGH)  4.14 us
    dot_general x8, matrix products, expect_sums(): sum_a = jnp.einsum('kn,nm->km', shares_block, ratio_alt, precision=HIGH)  2.96 us

profile of v1, /device:TPU:0, one launch (start us, length us, event | category | flops | bytes accessed | tf_op | source)
XLA Modules:
  0.0 146.5 jit_solution(7675783077697571270)
XLA Ops:
  0.6 0.8 reduce_sum.45
  1.4 6.2 %all_gather.12 = f32[12,1024]{1,0:T(8,128)S(1)} all-gather(f32[12,256]{1,0:T(8,128)S(1)} %broadcast_divide_fusion), channel_id=1, replica_groups=mesh['smp'=8,'var'=4] {'var'}, dimensions={1}, use_global_device_ids=true | all-gather | bytes 61440 | tf_op jit(solution)/shard_map/all_gather | solution.py:64
  7.7 0.7 copy-done.2
  8.4 31.4 %all-gather = f32[8,64,12]{1,2,0:T(8,128)S(1)} all-gather(f32[1,64,12]{1,2,0:T(8,128)S(1)} %bitcast.161), channel_id=1, replica_groups=mesh['smp'=8,'var'=4] {'smp'}, dimensions={0}, use_global_device_ids=true | all-gather | bytes 27648 | tf_op jit(solution)/shard_map/all_gather | solution.py:65
  39.9 0.8 copy-done
  40.7 10.8 %while.30 = (s32[]{:T(128)}, f32[12,512]{1,0:T(8,128)S(1)}, f32[12,512]{1,0:T(8,128)S(1)}, f32[4,12,256]{2,1,0:T(8,128)S(1)}, f32[4,12,256]{2,1,0:T(8,128)S(1)},...) while((s32[]{:T(128)}, f32[12,512]{1,0:T(8,128)S(1)}, ...), condition=%wide.region_2.3_spmd.clone, body=%wide.region_1.2_spmd.clone.sunk | while | flops 95716368 | bytes 3547396 | solution.py:43
  40.8 0.8 fusion.92
  41.6 0.4 convolution_add_fusion.10
  41.9 0.4 convolution_add_fusion.11
  42.3 0.5 convolution_bitcast_fusion.4
  42.8 0.5 fusion.93
  43.5 0.8 fusion.92
  44.2 0.4 convolution_add_fusion.10
  44.6 0.4 convolution_add_fusion.11
  45.0 0.5 convolution_bitcast_fusion.4
  45.5 0.5 fusion.93
  46.2 0.8 fusion.92
  46.9 0.4 convolution_add_fusion.10
  47.3 0.4 convolution_add_fusion.11
  47.7 0.5 convolution_bitcast_fusion.4
  48.2 0.5 fusion.93
  48.8 0.8 fusion.92
  49.6 0.4 convolution_add_fusion.10
  50.4 0.5 convolution_bitcast_fusion.4
  50.9 0.5 fusion.93
  51.5 5.8 %all_gather.14 = f32[4,12,1024]{2,1,0:T(8,128)S(1)} all-gather(f32[1,12,1024]{2,1,0:T(8,128)S(1)} %all_gather_reshape.6), channel_id=1, replica_groups=mesh['smp'=8,'var'=4] {'var'}, dimensions={0}, use_global_device_ids=true | all-gather | bytes 245760 | tf_op jit(solution)/shard_map/all_gather | solution.py:68
  57.4 37.5 %all-reduce.1 = (f32[12,512]{1,0:T(8,128)S(1)}, f32[12,512]{1,0:T(8,128)S(1)}) all-reduce(f32[12,512]{1,0:T(8,128)S(1)} %get-tuple-element.82, f32[12,512]{1,0:T(8,128)S(1)} %get-tuple-element.81), channel_id=1, replica_groups=mesh['smp'=8,'var'=4] {'smp'}, use_global_device_ids=true, to_apply=%region_6.7 | all-reduce | flops 12288 | bytes 98304 | tf_op jit(solution)/shard_map/psum | solution.py:69
  95.0 10.8 %while.31 = (s32[]{:T(128)}, f32[12,512]{1,0:T(8,128)S(1)}, f32[12,512]{1,0:T(8,128)S(1)}, f32[4,12,256]{2,1,0:T(8,128)S(1)}, f32[4,12,256]{2,1,0:T(8,128)S(1)},...) while((s32[]{:T(128)}, f32[12,512]{1,0:T(8,128)S(1)}, ...), condition=%wide.region_8.9_spmd.clone, body=%wide.region_7.8_spmd.clone.sunk | while | flops 95716368 | bytes 3547396 | solution.py:43
  95.1 0.8 fusion.103
  95.9 0.4 convolution_add_fusion.12
  96.7 0.5 convolution_bitcast_fusion.5
  97.2 0.5 fusion.104
  97.8 0.8 fusion.103
  98.6 0.4 convolution_add_fusion.12
  99.4 0.5 convolution_bitcast_fusion.5
  99.9 0.5 fusion.104
  100.5 0.8 fusion.103
  101.3 0.4 convolution_add_fusion.12
  102.1 0.5 convolution_bitcast_fusion.5
  102.6 0.5 fusion.104
  103.2 0.8 fusion.103
  104.0 0.4 convolution_add_fusion.12
  104.7 0.5 convolution_bitcast_fusion.5
  105.3 0.5 fusion.104
  105.9 5.8 %all_gather.15 = f32[4,12,1024]{2,1,0:T(8,128)S(1)} all-gather(f32[1,12,1024]{2,1,0:T(8,128)S(1)} %all_gather_reshape.7), channel_id=1, replica_groups=mesh['smp'=8,'var'=4] {'var'}, dimensions={0}, use_global_device_ids=true | all-gather | bytes 245760 | tf_op jit(solution)/shard_map/all_gather | solution.py:68
  111.8 0.6 fusion.44
  112.4 33.4 %all-reduce = (f32[12,512]{1,0:T(8,128)S(1)}, f32[12,512]{1,0:T(8,128)S(1)}) all-reduce(f32[12,512]{1,0:T(8,128)S(1)} %get-tuple-element.85, f32[12,512]{1,0:T(8,128)S(1)} %get-tuple-element.84), channel_id=1, replica_groups=mesh['smp'=8,'var'=4] {'smp'}, use_global_device_ids=true, to_apply=%region_12.13 | all-reduce | flops 12288 | bytes 98304 | tf_op jit(solution)/shard_map/psum | solution.py:69
  145.8 0.7 fusion.47
  (67 shorter events, 3.2 us)
Async XLA Ops:
  0.6 0.8 copy-start.1
  7.7 0.7 copy-start.2
  39.8 0.9 copy-start
